TPU v7x, 32 devices: a whole 2x2x4 slice. The times are simulated.
32 devices in a mesh: row: 4 (over x, core), theta: 4 (over z), phi: 2 (over y).
Axes of the slice: x: 2, y: 2, z: 4, core: 2. Of those that a mesh axis runs over, the one named last changes fastest.
Arguments:
- magnetic: float32 [3, 48, 64, 256], P(None, 'row', 'theta', 'phi'), may hold values from -6 to 6
- electric: float32 [3, 48, 64, 256], P(None, 'row', 'theta', 'phi'), may hold values from -6 to 6
Outputs:
- magnetic_new: float32 [3, 48, 64, 256], P(None, 'row', 'theta', 'phi')
- electric_new: float32 [3, 48, 64, 256], P(None, 'row', 'theta', 'phi')
All inputs are finite; a program needn't handle non-finite values.
Results may differ from a plain program's by a relative error of at most 0.0001.
Values sent between devices are 32-bit elements; how exact they have to be, the bound alone decides.
A program may use at most 64 MiB of HBM per device.

v0:
```python
import math

import jax
import jax.numpy as jnp
from jax import lax
from jax.sharding import PartitionSpec as P

hole_mass = 1.0
inner_radius = 1.8
wave_speed = 1.25
courant = 0.3
smooth_eps = 1e-06


def padded_2(block, sides, width, periodic):
    for axis, dim in sides:
        count = lax.axis_size(axis)
        forward = [(i, i + 1) for i in range(count - 1)]
        if periodic:
            forward.append((count - 1, 0))
        backward = [(target, source) for source, target in forward]
        low = lax.ppermute(
            lax.slice_in_dim(block, block.shape[dim] - width, None, axis=dim), axis, forward
        )
        high = lax.ppermute(lax.slice_in_dim(block, 0, width, axis=dim), axis, backward)
        block = jnp.concatenate([low, block, high], axis=dim)
    return block


def from_behind(array, axis, by):
    length = lax.axis_size(axis)
    return lax.ppermute(array, axis, [(i, (i + by) % length) for i in range(length)])


def weno_face(far_left, near_left, center, near_right, far_right):
    cand_low = (2.0 * far_left - 7.0 * near_left + 11.0 * center) / 6.0
    cand_mid = (-near_left + 5.0 * center + 2.0 * near_right) / 6.0
    cand_high = (2.0 * center + 5.0 * near_right - far_right) / 6.0
    rough_low = (
        13.0 / 12.0 * (far_left - 2.0 * near_left + center) ** 2
        + 0.25 * (far_left - 4.0 * near_left + 3.0 * center) ** 2
    )
    rough_mid = (
        13.0 / 12.0 * (near_left - 2.0 * center + near_right) ** 2
        + 0.25 * (near_left - near_right) ** 2
    )
    rough_high = (
        13.0 / 12.0 * (center - 2.0 * near_right + far_right) ** 2
        + 0.25 * (3.0 * center - 4.0 * near_right + far_right) ** 2
    )
    alpha_low = 0.1 / (smooth_eps + rough_low) ** 2
    alpha_mid = 0.6 / (smooth_eps + rough_mid) ** 2
    alpha_high = 0.3 / (smooth_eps + rough_high) ** 2
    return (alpha_low * cand_low + alpha_mid * cand_mid + alpha_high * cand_high) / (
        alpha_low + alpha_mid + alpha_high
    )


def interface(flux, field, axis):
    faces = flux.shape[axis] - 5
    plus_part = 0.5 * (flux + wave_speed * field)
    minus_part = 0.5 * (flux - wave_speed * field)
    plus_cuts = [
        lax.slice_in_dim(plus_part, offset, offset + faces, axis=axis) for offset in range(6)
    ]
    minus_cuts = [
        lax.slice_in_dim(minus_part, offset, offset + faces, axis=axis) for offset in range(6)
    ]
    left_state = weno_face(plus_cuts[0], plus_cuts[1], plus_cuts[2], plus_cuts[3], plus_cuts[4])
    right_state = weno_face(
        minus_cuts[5], minus_cuts[4], minus_cuts[3], minus_cuts[2], minus_cuts[1]
    )
    return left_state + right_state


def face_fluxes(fluxes, fields, axis):
    return lax.map(lambda couple: interface(couple[0], couple[1], axis), (fluxes, fields))


def tendency(padded, radii, angles, spacing_r, spacing_theta, spacing_phi):
    ratio = 2.0 * hole_mass / radii
    lapse_factor = (1.0 / jnp.sqrt(1.0 + ratio))[:, None, None]
    shift_speed = (ratio / (1.0 + ratio))[:, None, None]
    b_radial, b_polar, b_azimuth = (padded[0], padded[1], padded[2])
    d_radial, d_polar, d_azimuth = (padded[3], padded[4], padded[5])
    e_radial = lapse_factor * d_radial
    e_polar = lapse_factor * d_polar - shift_speed * b_azimuth
    e_azimuth = lapse_factor * d_azimuth + shift_speed * b_polar
    h_radial = lapse_factor * b_radial
    h_polar = lapse_factor * b_polar + shift_speed * d_azimuth
    h_azimuth = lapse_factor * b_azimuth - shift_speed * d_polar
    zeros_field = jnp.zeros_like(b_radial)
    radial_flux = jnp.stack([zeros_field, -e_azimuth, e_polar, zeros_field, h_azimuth, -h_polar])
    polar_flux = jnp.stack([e_azimuth, zeros_field, -e_radial, -h_azimuth, zeros_field, h_radial])
    azimuth_flux = jnp.stack([-e_polar, e_radial, zeros_field, h_polar, -h_radial, zeros_field])
    radial_faces = face_fluxes(radial_flux[:, :, 3:-3, 3:-3], padded[:, :, 3:-3, 3:-3], 0)
    polar_faces = face_fluxes(polar_flux[:, 3:-3, :, 3:-3], padded[:, 3:-3, :, 3:-3], 1)
    azimuth_faces = face_fluxes(azimuth_flux[:, 3:-3, 3:-3, :], padded[:, 3:-3, 3:-3, :], 2)
    radius_face = (0.5 * (radii[2:-3] + radii[3:-2])) ** 2
    radius_cell = radii[3:-3] ** 2
    sine_face = jnp.sin(0.5 * (angles[2:-3] + angles[3:-2]))
    sine_cell = jnp.sin(angles[3:-3])
    radial_div = (
        radius_face[None, 1:, None, None] * radial_faces[:, 1:]
        - radius_face[None, :-1, None, None] * radial_faces[:, :-1]
    ) / (radius_cell[None, :, None, None] * spacing_r)
    polar_div = (
        sine_face[None, None, 1:, None] * polar_faces[:, :, 1:]
        - sine_face[None, None, :-1, None] * polar_faces[:, :, :-1]
    ) / (sine_cell[None, None, :, None] * spacing_theta)
    azimuth_div = (azimuth_faces[:, :, :, 1:] - azimuth_faces[:, :, :, :-1]) / spacing_phi
    return -(radial_div + polar_div + azimuth_div)


def project(fields):
    magnetic_part = fields[:3]
    electric_part = fields[3:]
    b_square = jnp.maximum(jnp.sum(magnetic_part * magnetic_part, axis=0), 1.0)
    along = jnp.sum(magnetic_part * electric_part, axis=0) / b_square
    electric_part = electric_part - along[None] * magnetic_part
    d_square = jnp.sum(electric_part * electric_part, axis=0)
    shrink = jnp.sqrt(b_square / jnp.maximum(d_square, b_square))
    return jnp.concatenate([magnetic_part, electric_part * shrink[None]], axis=0)


def body(magnetic, electric):
    fields = jnp.concatenate([magnetic, electric], axis=0)
    rows_dev = fields.shape[1]
    theta_dev = fields.shape[2]
    n_theta = lax.axis_size("theta")
    n_phi = lax.axis_size("phi")
    n_row = lax.axis_size("row")
    total_rows = rows_dev * n_row
    spacing_theta = math.pi / (theta_dev * n_theta)
    spacing_phi = 2.0 * math.pi / (fields.shape[3] * n_phi)
    step_dt = courant / (1.0 / spacing_theta + 1.0 / spacing_theta + 1.0 / spacing_phi)
    row_start = lax.axis_index("row") * rows_dev
    theta_index = lax.axis_index("theta")
    angles = (
        (theta_index * theta_dev - 3 + jnp.arange(theta_dev + 6)).astype(jnp.float32) + 0.5
    ) * spacing_theta
    parity = jnp.array([1.0, -1.0, -1.0, 1.0, -1.0, -1.0], jnp.float32)[:, None, None, None]
    weights = (0.0, 0.75, 1.0 / 3.0)
    current = fields
    for section_index in range(3):
        extended = padded_2(current, (("phi", 3),), 3, True)
        extended = padded_2(extended, (("row", 1),), 3, False)
        polar_padded = padded_2(extended, (("theta", 2),), 3, False)
        north_rows = polar_padded[:, :, 5:2:-1, :]
        south_rows = polar_padded[:, :, -4:-7:-1, :]
        outgoing = jnp.where(theta_index == 0, north_rows, south_rows)
        incoming = from_behind(outgoing, "phi", n_phi // 2)
        upper_ghost = jnp.where(theta_index == 0, incoming * parity, polar_padded[:, :, :3])
        lower_ghost = jnp.where(
            theta_index == n_theta - 1, incoming * parity, polar_padded[:, :, -3:]
        )
        weight = weights[section_index]
        global_rows = row_start - 3 + jnp.arange(rows_dev + 2 * 3)
        radii = inner_radius + (global_rows.astype(jnp.float32) + 0.5) * spacing_theta
        rates = tendency(
            jnp.concatenate([upper_ghost, polar_padded[:, :, 3:-3], lower_ghost], axis=2),
            radii,
            angles,
            spacing_theta,
            spacing_theta,
            spacing_phi,
        )
        updated = project(weight * fields + (1.0 - weight) * (current + step_dt * rates))
        kept_rows = global_rows[3:-3]
        inside = (kept_rows >= 0) & (kept_rows < total_rows)
        current = jnp.where(inside[None, :, None, None], updated, 0.0)
    return (current[:3], current[3:])


def solution(mesh):
    in_specs = (P(None, "row", "theta", "phi"), P(None, "row", "theta", "phi"))
    out_specs = (P(None, "row", "theta", "phi"), P(None, "row", "theta", "phi"))
    return jax.shard_map(body, mesh=mesh, in_specs=in_specs, out_specs=out_specs, check_vma=False)
```

profile of v0, /device:TPU:0, one launch (start us, length us, event | category | flops | bytes accessed | tf_op | source)
XLA Modules:
  0.0 312.7 jit_solution(1438143854139053936)
XLA Ops:
  3.5 3.1 collective-permute-start
  8.8 2.5 collective-permute-done
  19.5 2.9 collective-permute-done.3
  24.6 4.2 %collective-permute-start.5 = (f32[6,18,3,134]{3,1,2,0:T(8,128)}, f32[6,18,3,134]{3,1,2,0:T(8,128)}, u32[]{:S(2)}, u32[]{:S(2)}) collective-permute-start(f32[6,18,3,134]{3,1,2,0:T(8,128)} %copy.242), channel_id=1, source_target_pairs={{0,2},{2,4},{4,6},{1,3},{3,5},{5,7},{8,10},{10,12},{12,14},{9,11},... | collective-permute-start | bytes 521000 | tf_op jit(solution)/shard_map/ppermute | solution.py:22
  35.0 6.8 %collective-permute-done.4 = f32[6,18,3,134]{3,1,2,0:T(8,128)} collective-permute-done((f32[6,18,3,134]{3,1,2,0:T(8,128)}, f32[6,18,3,134]{3,1,2,0:T(8,128)}, u32[]{:S(2)}, u32[]{:S(2)}) %collective-permute-start.4) | collective-permute-done | bytes 173696 | tf_op jit(solution)/shard_map/ppermute | solution.py:32
  49.9 8.3 %while.90 = (s32[]{:T(128)}, f32[6,13,16,128]{3,2,1,0:T(8,128)S(1)}, f32[6,18,16,128]{3,2,1,0:T(8,128)S(1)}, f32[6,18,16,128]{3,2,1,0:T(8,128)}, s32[]{:T(128)}) while((s32[]{:T(128)}, f32[6,13,16,128]{3,2,1,0:T(8,128)S(1)}, f32[6,18,16,128]{3,2,1,0:T(8,128)S(1)}, f32[6,18,16,128]{3,2,1,0:T(8,128)}, s32[]{:T(128)}) %tuple.213), condition=%wide.region_1.2_spmd, body=%wide.region_0.1_spmd.sunk | while | flops 3618818 | bytes 1761349 | solution.py:77
  61.2 2.7 slice.841
  64.0 10.7 %while.91 = (s32[]{:T(128)}, f32[6,12,17,128]{3,2,1,0:T(8,128)S(1)}, f32[6,12,22,128]{3,2,1,0:T(8,128)}, f32[6,12,22,128]{3,2,1,0:T(8,128)}, s32[]{:T(128)}) while((s32[]{:T(128)}, f32[6,12,17,128]{3,2,1,0:T(8,128)S(1)}, f32[6,12,22,128]{3,2,1,0:T(8,128)}, f32[6,12,22,128]{3,2,1,0:T(8,128)}, s32[]{:T(128)}) %tuple.210), condition=%wide.region_3.4_spmd, body=%wide.region_2.3_spmd.sunk | while | flops 3537410 | bytes 2162757 | solution.py:77
  75.5 2.7 slice.843
  79.4 16.1 %while.92 = (s32[]{:T(128)}, f32[6,12,16,129]{3,2,1,0:T(8,128)}, f32[6,12,16,134]{3,2,1,0:T(8,128)}, f32[6,12,16,134]{3,2,1,0:T(8,128)S(1)}, s32[]{:T(128)}) while((s32[]{:T(128)}, f32[6,12,16,129]{3,2,1,0:T(8,128)}, f32[6,12,16,134]{3,2,1,0:T(8,128)}, f32[6,12,16,134]{3,2,1,0:T(8,128)S(1)}, s32[]{:T(128)}) %tuple.207), condition=%wide.region_5.6_spmd, body=%wide.region_4.5_spmd.sunk | while | flops 3323714 | bytes 1599553 | solution.py:77
  101.9 2.4 collective-permute-done.7
  104.8 2.9 collective-permute-done.8
  110.1 4.4 %collective-permute-start.9 = (f32[6,3,16,134]{3,2,1,0:T(8,128)S(1)}, f32[6,3,16,134]{3,2,1,0:T(8,128)S(1)}, u32[]{:S(2)}, u32[]{:S(2)}) collective-permute-start(f32[6,3,16,134]{3,2,1,0:T(8,128)S(1)} %get-tuple-element.385), channel_id=1, source_target_pairs={{0,8},{8,16},{16,24},{1,9},{9,17},{17,25},{2,10},{10,18},{18,26},{... | collective-permute-start | bytes 463112 | tf_op jit(solution)/shard_map/ppermute | solution.py:22
  117.9 5.7 %collective-permute-start.12 = (f32[6,18,3,134]{3,1,2,0:T(8,128)}, f32[6,18,3,134]{3,1,2,0:T(8,128)}, u32[]{:S(2)}, u32[]{:S(2)}) collective-permute-start(f32[6,18,3,134]{3,1,2,0:T(8,128)} %copy.244), channel_id=1, source_target_pairs={{0,2},{2,4},{4,6},{1,3},{3,5},{5,7},{8,10},{10,12},{12,14},{9,11},... | collective-permute-start | bytes 521000 | tf_op jit(solution)/shard_map/ppermute | solution.py:22
  131.0 6.5 %collective-permute-done.11 = f32[6,18,3,134]{3,1,2,0:T(8,128)} collective-permute-done((f32[6,18,3,134]{3,1,2,0:T(8,128)}, f32[6,18,3,134]{3,1,2,0:T(8,128)}, u32[]{:S(2)}, u32[]{:S(2)}) %collective-permute-start.11) | collective-permute-done | bytes 173696 | tf_op jit(solution)/shard_map/ppermute | solution.py:32
  147.0 12.5 %while.93 = (s32[]{:T(128)}, f32[6,13,16,128]{3,2,1,0:T(8,128)}, f32[6,18,16,128]{3,2,1,0:T(8,128)}, f32[6,18,16,128]{3,2,1,0:T(8,128)}, s32[]{:T(128)}) while((s32[]{:T(128)}, f32[6,13,16,128]{3,2,1,0:T(8,128)}, f32[6,18,16,128]{3,2,1,0:T(8,128)}, f32[6,18,16,128]{3,2,1,0:T(8,128)}, s32[]{:T(128)}) %tuple.222), condition=%wide.region_10.11_spmd, body=%wide.region_9.10_spmd.sunk | while | flops 3618818 | bytes 1761857 | solution.py:77
  162.5 2.7 slice.857
  166.2 14.6 %while.94 = (s32[]{:T(128)}, f32[6,12,17,128]{3,2,1,0:T(8,128)}, f32[6,12,22,128]{3,2,1,0:T(8,128)}, f32[6,12,22,128]{3,2,1,0:T(8,128)}, s32[]{:T(128)}) while((s32[]{:T(128)}, f32[6,12,17,128]{3,2,1,0:T(8,128)}, f32[6,12,22,128]{3,2,1,0:T(8,128)}, f32[6,12,22,128]{3,2,1,0:T(8,128)}, s32[]{:T(128)}) %tuple.219), condition=%wide.region_12.13_spmd, body=%wide.region_11.12_spmd.sunk | while | flops 3537410 | bytes 1733185 | solution.py:77
  181.6 2.7 slice.859
  185.5 16.1 %while.95 = (s32[]{:T(128)}, f32[6,12,16,129]{3,2,1,0:T(8,128)}, f32[6,12,16,134]{3,2,1,0:T(8,128)}, f32[6,12,16,134]{3,2,1,0:T(8,128)S(1)}, s32[]{:T(128)}) while((s32[]{:T(128)}, f32[6,12,16,129]{3,2,1,0:T(8,128)}, f32[6,12,16,134]{3,2,1,0:T(8,128)}, f32[6,12,16,134]{3,2,1,0:T(8,128)S(1)}, s32[]{:T(128)}) %tuple.216), condition=%wide.region_14.15_spmd, body=%wide.region_13.14_spmd.sunk | while | flops 3323714 | bytes 1599553 | solution.py:77
  201.6 2.8 multiply_add_fusion.1
  211.8 2.4 collective-permute-done.15
  215.3 3.5 %collective-permute-start.16 = (f32[6,3,16,134]{3,2,1,0:T(8,128)S(1)}, f32[6,3,16,134]{3,2,1,0:T(8,128)S(1)}, u32[]{:S(2)}, u32[]{:S(2)}) collective-permute-start(f32[6,3,16,134]{3,2,1,0:T(8,128)S(1)} %get-tuple-element.383), channel_id=1, source_target_pairs={{0,8},{8,16},{16,24},{1,9},{9,17},{17,25},{2,10},{10,18},{18,26},{... | collective-permute-start | bytes 463112 | tf_op jit(solution)/shard_map/ppermute | solution.py:22
  220.2 3.5 %collective-permute-done.17 = f32[6,3,16,134]{3,2,1,0:T(8,128)S(1)} collective-permute-done((f32[6,3,16,134]{3,2,1,0:T(8,128)S(1)}, f32[6,3,16,134]{3,2,1,0:T(8,128)S(1)}, u32[]{:S(2)}, u32[]{:S(2)}) %collective-permute-start.17) | collective-permute-done | bytes 154400 | tf_op jit(solution)/shard_map/ppermute | solution.py:25
  226.0 5.1 %collective-permute-start.19 = (f32[6,18,3,134]{3,1,2,0:T(8,128)}, f32[6,18,3,134]{3,1,2,0:T(8,128)}, u32[]{:S(2)}, u32[]{:S(2)}) collective-permute-start(f32[6,18,3,134]{3,1,2,0:T(8,128)} %copy.246), channel_id=1, source_target_pairs={{0,2},{2,4},{4,6},{1,3},{3,5},{5,7},{8,10},{10,12},{12,14},{9,11},... | collective-permute-start | bytes 521000 | tf_op jit(solution)/shard_map/ppermute | solution.py:22
  238.9 5.3 %collective-permute-done.18 = f32[6,18,3,134]{3,1,2,0:T(8,128)} collective-permute-done((f32[6,18,3,134]{3,1,2,0:T(8,128)}, f32[6,18,3,134]{3,1,2,0:T(8,128)}, u32[]{:S(2)}, u32[]{:S(2)}) %collective-permute-start.18) | collective-permute-done | bytes 173696 | tf_op jit(solution)/shard_map/ppermute | solution.py:32
  253.7 12.5 %while.96 = (s32[]{:T(128)}, f32[6,13,16,128]{3,2,1,0:T(8,128)}, f32[6,18,16,128]{3,2,1,0:T(8,128)}, f32[6,18,16,128]{3,2,1,0:T(8,128)}, s32[]{:T(128)}) while((s32[]{:T(128)}, f32[6,13,16,128]{3,2,1,0:T(8,128)}, f32[6,18,16,128]{3,2,1,0:T(8,128)}, f32[6,18,16,128]{3,2,1,0:T(8,128)}, s32[]{:T(128)}) %tuple.231), condition=%wide.region_19.20_spmd, body=%wide.region_18.19_spmd.sunk | while | flops 3618818 | bytes 1761857 | solution.py:77
  269.2 2.7 slice.873
  272.9 14.6 %while.97 = (s32[]{:T(128)}, f32[6,12,17,128]{3,2,1,0:T(8,128)}, f32[6,12,22,128]{3,2,1,0:T(8,128)}, f32[6,12,22,128]{3,2,1,0:T(8,128)}, s32[]{:T(128)}) while((s32[]{:T(128)}, f32[6,12,17,128]{3,2,1,0:T(8,128)}, f32[6,12,22,128]{3,2,1,0:T(8,128)}, f32[6,12,22,128]{3,2,1,0:T(8,128)}, s32[]{:T(128)}) %tuple.228), condition=%wide.region_21.22_spmd, body=%wide.region_20.21_spmd.sunk | while | flops 3537410 | bytes 1733185 | solution.py:77
  288.3 2.7 slice.875
  292.2 16.1 %while.98 = (s32[]{:T(128)}, f32[6,12,16,129]{3,2,1,0:T(8,128)}, f32[6,12,16,134]{3,2,1,0:T(8,128)}, f32[6,12,16,134]{3,2,1,0:T(8,128)S(1)}, s32[]{:T(128)}) while((s32[]{:T(128)}, f32[6,12,16,129]{3,2,1,0:T(8,128)}, f32[6,12,16,134]{3,2,1,0:T(8,128)}, f32[6,12,16,134]{3,2,1,0:T(8,128)S(1)}, s32[]{:T(128)}) %tuple.225), condition=%wide.region_23.24_spmd, body=%wide.region_22.23_spmd.sunk | while | flops 3323714 | bytes 1599553 | solution.py:77
  308.3 2.8 multiply_add_fusion
  (335 shorter events, 227.5 us)
Async XLA Ops:
  3.5 7.8 %collective-permute-start = (f32[6,12,16,3]{2,1,3,0:T(8,128)S(1)}, f32[6,12,16,3]{2,1,3,0:T(8,128)S(1)}, u32[]{:S(2)}, u32[]{:S(2)}) collective-permute-start(f32[6,12,16,3]{2,1,3,0:T(8,128)S(1)} %copy.239), channel_id=1, source_target_pairs={{0,1},{1,0},{2,3},{3,2},{4,5},{5,4},{6,7},{7,6},{8,9},{9,8},{10,11... | collective-permute-start | bytes 41480 | tf_op jit(solution)/shard_map/ppermute | solution.py:22
  7.2 6.3 %collective-permute-start.1 = (f32[6,12,16,3]{2,1,3,0:T(8,128)S(1)}, f32[6,12,16,3]{2,1,3,0:T(8,128)S(1)}, u32[]{:S(2)}, u32[]{:S(2)}) collective-permute-start(f32[6,12,16,3]{2,1,3,0:T(8,128)S(1)} %copy.240), channel_id=1, source_target_pairs={{1,0},{0,1},{3,2},{2,3},{5,4},{4,5},{7,6},{6,7},{9,8},{8,9},{11,10... | collective-permute-start | bytes 41480 | tf_op jit(solution)/shard_map/ppermute | solution.py:25
  15.4 4.0 %collective-permute-start.2 = (f32[6,3,16,134]{3,2,1,0:T(8,128)}, f32[6,3,16,134]{3,2,1,0:T(8,128)S(1)}, u32[]{:S(2)}, u32[]{:S(2)}) collective-permute-start(f32[6,3,16,134]{3,2,1,0:T(8,128)} %get-tuple-element.387), channel_id=1, source_target_pairs={{0,8},{8,16},{16,24},{1,9},{9,17},{17,25},{2,10},{10,18},{18,26},{... | collective-permute-start | bytes 463112 | tf_op jit(solution)/shard_map/ppermute | solution.py:22
  16.7 5.6 %collective-permute-start.3 = (f32[6,3,16,134]{3,2,1,0:T(8,128)}, f32[6,3,16,134]{3,2,1,0:T(8,128)S(1)}, u32[]{:S(2)}, u32[]{:S(2)}) collective-permute-start(f32[6,3,16,134]{3,2,1,0:T(8,128)} %get-tuple-element.388), channel_id=1, source_target_pairs={{8,0},{16,8},{24,16},{9,1},{17,9},{25,17},{10,2},{18,10},{26,18},{... | collective-permute-start | bytes 463112 | tf_op jit(solution)/shard_map/ppermute | solution.py:25
  24.6 17.2 %collective-permute-start.5 = (f32[6,18,3,134]{3,1,2,0:T(8,128)}, f32[6,18,3,134]{3,1,2,0:T(8,128)}, u32[]{:S(2)}, u32[]{:S(2)}) collective-permute-start(f32[6,18,3,134]{3,1,2,0:T(8,128)} %copy.242), channel_id=1, source_target_pairs={{0,2},{2,4},{4,6},{1,3},{3,5},{5,7},{8,10},{10,12},{12,14},{9,11},... | collective-permute-start | bytes 521000 | tf_op jit(solution)/shard_map/ppermute | solution.py:22
  28.8 13.0 %collective-permute-start.6 = (f32[6,18,3,134]{3,1,2,0:T(8,128)}, f32[6,18,3,134]{3,1,2,0:T(8,128)}, u32[]{:S(2)}, u32[]{:S(2)}) collective-permute-start(f32[6,18,3,134]{3,1,2,0:T(8,128)} %copy.241), channel_id=1, source_target_pairs={{2,0},{4,2},{6,4},{3,1},{5,3},{7,5},{10,8},{12,10},{14,12},{11,9},... | collective-permute-start | bytes 521000 | tf_op jit(solution)/shard_map/ppermute | solution.py:25
  32.3 9.5 %collective-permute-start.4 = (f32[6,18,3,134]{3,1,2,0:T(8,128)}, f32[6,18,3,134]{3,1,2,0:T(8,128)}, u32[]{:S(2)}, u32[]{:S(2)}) collective-permute-start(f32[6,18,3,134]{3,1,2,0:T(8,128)} %reverse_select_fusion.2), channel_id=1, source_target_pairs={{0,1},{1,0},{2,3},{3,2},{4,5},{5,4},{6,7},{7,6},{8,9},{9,8},{10,11... | collective-permute-start | bytes 521000 | tf_op jit(solution)/shard_map/ppermute | solution.py:32
  79.4 16.1 %copy-start.20 = (f32[12]{0:T(128)S(1)}, f32[12]{0:T(128)}, u32[]{:S(2)}) copy-start(f32[12]{0:T(128)} %get-tuple-element.416) | copy-start | bytes 148
  79.4 16.1 %copy-start.23 = (f32[16]{0:T(128)S(1)}, f32[16]{0:T(128)}, u32[]{:S(2)}) copy-start(f32[16]{0:T(128)} %get-tuple-element.411) | copy-start | bytes 196
  79.4 16.1 %copy-start.26 = (f32[16]{0:T(128)S(1)}, f32[16]{0:T(128)}, u32[]{:S(2)}) copy-start(f32[16]{0:T(128)} %get-tuple-element.412) | copy-start | bytes 196
  79.4 16.1 %copy-start.29 = (f32[16]{0:T(128)S(1)}, f32[16]{0:T(128)}, u32[]{:S(2)}) copy-start(f32[16]{0:T(128)} %get-tuple-element.415) | copy-start | bytes 196
  99.1 5.2 %collective-permute-start.7 = (f32[6,12,16,3]{2,1,3,0:T(8,128)S(1)}, f32[6,12,16,3]{2,1,3,0:T(8,128)S(1)}, u32[]{:S(2)}, u32[]{:S(2)}) collective-permute-start(f32[6,12,16,3]{2,1,3,0:T(8,128)S(1)} %copy.223), channel_id=1, source_target_pairs={{0,1},{1,0},{2,3},{3,2},{4,5},{5,4},{6,7},{7,6},{8,9},{9,8},{10,11... | collective-permute-start | bytes 41480 | tf_op jit(solution)/shard_map/ppermute | solution.py:22
  101.4 6.4 %collective-permute-start.8 = (f32[6,12,16,3]{2,1,3,0:T(8,128)S(1)}, f32[6,12,16,3]{2,1,3,0:T(8,128)S(1)}, u32[]{:S(2)}, u32[]{:S(2)}) collective-permute-start(f32[6,12,16,3]{2,1,3,0:T(8,128)S(1)} %copy.224), channel_id=1, source_target_pairs={{1,0},{0,1},{3,2},{2,3},{5,4},{4,5},{7,6},{6,7},{9,8},{8,9},{11,10... | collective-permute-start | bytes 41480 | tf_op jit(solution)/shard_map/ppermute | solution.py:25
  108.8 5.7 %collective-permute-start.10 = (f32[6,3,16,134]{3,2,1,0:T(8,128)S(1)}, f32[6,3,16,134]{3,2,1,0:T(8,128)S(1)}, u32[]{:S(2)}, u32[]{:S(2)}) collective-permute-start(f32[6,3,16,134]{3,2,1,0:T(8,128)S(1)} %get-tuple-element.386), channel_id=1, source_target_pairs={{8,0},{16,8},{24,16},{9,1},{17,9},{25,17},{10,2},{18,10},{26,18},{... | collective-permute-start | bytes 463112 | tf_op jit(solution)/shard_map/ppermute | solution.py:25
  110.1 5.6 %collective-permute-start.9 = (f32[6,3,16,134]{3,2,1,0:T(8,128)S(1)}, f32[6,3,16,134]{3,2,1,0:T(8,128)S(1)}, u32[]{:S(2)}, u32[]{:S(2)}) collective-permute-start(f32[6,3,16,134]{3,2,1,0:T(8,128)S(1)} %get-tuple-element.385), channel_id=1, source_target_pairs={{0,8},{8,16},{16,24},{1,9},{9,17},{17,25},{2,10},{10,18},{18,26},{... | collective-permute-start | bytes 463112 | tf_op jit(solution)/shard_map/ppermute | solution.py:22
  117.9 19.7 %collective-permute-start.12 = (f32[6,18,3,134]{3,1,2,0:T(8,128)}, f32[6,18,3,134]{3,1,2,0:T(8,128)}, u32[]{:S(2)}, u32[]{:S(2)}) collective-permute-start(f32[6,18,3,134]{3,1,2,0:T(8,128)} %copy.244), channel_id=1, source_target_pairs={{0,2},{2,4},{4,6},{1,3},{3,5},{5,7},{8,10},{10,12},{12,14},{9,11},... | collective-permute-start | bytes 521000 | tf_op jit(solution)/shard_map/ppermute | solution.py:22
  125.5 12.3 %collective-permute-start.13 = (f32[6,18,3,134]{3,1,2,0:T(8,128)}, f32[6,18,3,134]{3,1,2,0:T(8,128)}, u32[]{:S(2)}, u32[]{:S(2)}) collective-permute-start(f32[6,18,3,134]{3,1,2,0:T(8,128)} %copy.243), channel_id=1, source_target_pairs={{2,0},{4,2},{6,4},{3,1},{5,3},{7,5},{10,8},{12,10},{14,12},{11,9},... | collective-permute-start | bytes 521000 | tf_op jit(solution)/shard_map/ppermute | solution.py:25
  127.1 10.5 %collective-permute-start.11 = (f32[6,18,3,134]{3,1,2,0:T(8,128)}, f32[6,18,3,134]{3,1,2,0:T(8,128)}, u32[]{:S(2)}, u32[]{:S(2)}) collective-permute-start(f32[6,18,3,134]{3,1,2,0:T(8,128)} %reverse_select_fusion.1), channel_id=1, source_target_pairs={{0,1},{1,0},{2,3},{3,2},{4,5},{5,4},{6,7},{7,6},{8,9},{9,8},{10,11... | collective-permute-start | bytes 521000 | tf_op jit(solution)/shard_map/ppermute | solution.py:32
  185.5 16.1 %copy-start.21 = (f32[12]{0:T(128)S(1)}, f32[12]{0:T(128)}, u32[]{:S(2)}) copy-start(f32[12]{0:T(128)} %get-tuple-element.416) | copy-start | bytes 148
  185.5 16.1 %copy-start.24 = (f32[16]{0:T(128)S(1)}, f32[16]{0:T(128)}, u32[]{:S(2)}) copy-start(f32[16]{0:T(128)} %get-tuple-element.411) | copy-start | bytes 196
  185.5 16.1 %copy-start.27 = (f32[16]{0:T(128)S(1)}, f32[16]{0:T(128)}, u32[]{:S(2)}) copy-start(f32[16]{0:T(128)} %get-tuple-element.412) | copy-start | bytes 196
  185.5 16.1 %copy-start.30 = (f32[16]{0:T(128)S(1)}, f32[16]{0:T(128)}, u32[]{:S(2)}) copy-start(f32[16]{0:T(128)} %get-tuple-element.415) | copy-start | bytes 196
  206.1 5.2 %collective-permute-start.14 = (f32[6,12,16,3]{2,1,3,0:T(8,128)S(1)}, f32[6,12,16,3]{2,1,3,0:T(8,128)S(1)}, u32[]{:S(2)}, u32[]{:S(2)}) collective-permute-start(f32[6,12,16,3]{2,1,3,0:T(8,128)S(1)} %copy.231), channel_id=1, source_target_pairs={{0,1},{1,0},{2,3},{3,2},{4,5},{5,4},{6,7},{7,6},{8,9},{9,8},{10,11... | collective-permute-start | bytes 41480 | tf_op jit(solution)/shard_map/ppermute | solution.py:22
  207.7 6.6 %collective-permute-start.15 = (f32[6,12,16,3]{2,1,3,0:T(8,128)S(1)}, f32[6,12,16,3]{2,1,3,0:T(8,128)S(1)}, u32[]{:S(2)}, u32[]{:S(2)}) collective-permute-start(f32[6,12,16,3]{2,1,3,0:T(8,128)S(1)} %copy.232), channel_id=1, source_target_pairs={{1,0},{0,1},{3,2},{2,3},{5,4},{4,5},{7,6},{6,7},{9,8},{8,9},{11,10... | collective-permute-start | bytes 41480 | tf_op jit(solution)/shard_map/ppermute | solution.py:25
  215.3 4.9 %collective-permute-start.16 = (f32[6,3,16,134]{3,2,1,0:T(8,128)S(1)}, f32[6,3,16,134]{3,2,1,0:T(8,128)S(1)}, u32[]{:S(2)}, u32[]{:S(2)}) collective-permute-start(f32[6,3,16,134]{3,2,1,0:T(8,128)S(1)} %get-tuple-element.383), channel_id=1, source_target_pairs={{0,8},{8,16},{16,24},{1,9},{9,17},{17,25},{2,10},{10,18},{18,26},{... | collective-permute-start | bytes 463112 | tf_op jit(solution)/shard_map/ppermute | solution.py:22
  218.9 4.9 %collective-permute-start.17 = (f32[6,3,16,134]{3,2,1,0:T(8,128)S(1)}, f32[6,3,16,134]{3,2,1,0:T(8,128)S(1)}, u32[]{:S(2)}, u32[]{:S(2)}) collective-permute-start(f32[6,3,16,134]{3,2,1,0:T(8,128)S(1)} %get-tuple-element.384), channel_id=1, source_target_pairs={{8,0},{16,8},{24,16},{9,1},{17,9},{25,17},{10,2},{18,10},{26,18},{... | collective-permute-start | bytes 463112 | tf_op jit(solution)/shard_map/ppermute | solution.py:25
  226.0 18.3 %collective-permute-start.19 = (f32[6,18,3,134]{3,1,2,0:T(8,128)}, f32[6,18,3,134]{3,1,2,0:T(8,128)}, u32[]{:S(2)}, u32[]{:S(2)}) collective-permute-start(f32[6,18,3,134]{3,1,2,0:T(8,128)} %copy.246), channel_id=1, source_target_pairs={{0,2},{2,4},{4,6},{1,3},{3,5},{5,7},{8,10},{10,12},{12,14},{9,11},... | collective-permute-start | bytes 521000 | tf_op jit(solution)/shard_map/ppermute | solution.py:22
  233.1 11.4 %collective-permute-start.20 = (f32[6,18,3,134]{3,1,2,0:T(8,128)}, f32[6,18,3,134]{3,1,2,0:T(8,128)}, u32[]{:S(2)}, u32[]{:S(2)}) collective-permute-start(f32[6,18,3,134]{3,1,2,0:T(8,128)} %copy.245), channel_id=1, source_target_pairs={{2,0},{4,2},{6,4},{3,1},{5,3},{7,5},{10,8},{12,10},{14,12},{11,9},... | collective-permute-start | bytes 521000 | tf_op jit(solution)/shard_map/ppermute | solution.py:25
  234.6 9.6 %collective-permute-start.18 = (f32[6,18,3,134]{3,1,2,0:T(8,128)}, f32[6,18,3,134]{3,1,2,0:T(8,128)}, u32[]{:S(2)}, u32[]{:S(2)}) collective-permute-start(f32[6,18,3,134]{3,1,2,0:T(8,128)} %reverse_select_fusion), channel_id=1, source_target_pairs={{0,1},{1,0},{2,3},{3,2},{4,5},{5,4},{6,7},{7,6},{8,9},{9,8},{10,11... | collective-permute-start | bytes 521000 | tf_op jit(solution)/shard_map/ppermute | solution.py:32
  292.2 16.1 %copy-start.25 = (f32[16]{0:T(128)S(1)}, f32[16]{0:T(128)}, u32[]{:S(2)}) copy-start(f32[16]{0:T(128)} %get-tuple-element.411) | copy-start | bytes 196
  292.2 16.1 %copy-start.28 = (f32[16]{0:T(128)S(1)}, f32[16]{0:T(128)}, u32[]{:S(2)}) copy-start(f32[16]{0:T(128)} %get-tuple-element.412) | copy-start | bytes 196
  292.2 16.1 %copy-start.31 = (f32[16]{0:T(128)S(1)}, f32[16]{0:T(128)}, u32[]{:S(2)}) copy-start(f32[16]{0:T(128)} %get-tuple-element.415) | copy-start | bytes 196
  (24 other events, 116.0 us)
where the time goes:
time: 318 us; the launch traced here: 313 us
  other arithmetic  162 us (51%)
  local copies, waits for them, and re-layouts  64.2 us (20%)
  starting transfers between devices  43.8 us (14%)
  waiting for transfers between devices  41.1 us (13%)
    dynamic_update_slice x54, other arithmetic, face_fluxes(): lax.map(lambda couple: interface(couple[0], couple[1], axis), (fluxes, fi...  67.4 us
    mul x54, other arithmetic, interface(): plus_part = 0.5 * (flux + wave_speed * field)  53.5 us
    ppermute x9, starting transfers between devices, padded_2(): lax.ppermute(lax.slice_in_dim(block, block.shape[dim] - width, None, axis...  29.9 us
    unnamed x94, local copies, waits for them, and re-layouts  20.4 us
    ppermute x3, waiting for transfers between devices, from_behind(): lax.ppermute(array, axis, [(i, (i + by) % length) for i in range(length)])  18.6 us
    ppermute x9, waiting for transfers between devices, padded_2(): lax.ppermute(lax.slice_in_dim(block, 0, width, axis=dim), axis, backward)  14.2 us
    ppermute x9, starting transfers between devices, padded_2(): lax.ppermute(lax.slice_in_dim(block, 0, width, axis=dim), axis, backward)  10.2 us
    ppermute x9, waiting for transfers between devices, padded_2(): lax.ppermute(lax.slice_in_dim(block, block.shape[dim] - width, None, axis...  8.4 us
  transfers between devices with their start and end apart: 21, of which 14 were waited for; matrix products, arithmetic and copies ran while one was open for 6% of the time, Pallas kernels for 0%

commit v1 on v0

v1 whole, which is shorter than its diff:
```python
import functools
import math

import jax
import jax.numpy as jnp
from jax import lax
from jax.experimental import pallas as pl
from jax.experimental.pallas import tpu as pltpu
from jax.sharding import PartitionSpec as P

MESH = pl.DeviceIdType.MESH
hole_mass = 1.0
inner_radius = 1.8
wave_speed = 1.25
courant = 0.3
smooth_eps = 1e-06
G = 3
ZERO = ((0, 3), (1, 4), (2, 5))


def flux_of(dim, u, a, s):
    b1, b2, b3, d1, d2, d3 = u
    if dim == 0:
        e2, e3 = a * d2 - s * b3, a * d3 + s * b2
        h2, h3 = a * b2 + s * d3, a * b3 - s * d2
        return [None, -e3, e2, None, h3, -h2]
    if dim == 1:
        e1, e3 = a * d1, a * d3 + s * b2
        h1, h3 = a * b1, a * b3 - s * d2
        return [e3, None, -e1, -h3, None, h1]
    e1, e2 = a * d1, a * d2 - s * b3
    h1, h2 = a * b1, a * b2 + s * d3
    return [-e2, e1, None, h2, -h1, None]


def split(dim, u, a, s):
    out = []
    for f, x in zip(flux_of(dim, u, a, s), u):
        k = wave_speed * x
        out.append((k, -k) if f is None else (f + k, f - k))
    return out


def correction(d0, d1, d2, d3):
    k, eps = 0.609375, 3.0 * smooth_eps
    r1 = (k * d1) * d1 + eps
    r2 = (k * d2) * d2 + eps
    x0 = d0 - 1.375 * d1
    x1 = d1 - 0.625 * d2
    x2 = d3 - 1.375 * d2
    s0, s1, s2 = x0 * x0 + r1, x1 * x1 + r2, x2 * x2 + r2
    s0, s1, s2 = s0 * s0, s1 * s1, s2 * s2
    z = 3.0 * s0
    n0, n2, y = s1 * s2, z * s1, z * s2
    den = (n0 + n2) + (y + y)
    t2 = d2 - d1
    t_low = t2 - (d1 - d0)
    t_high = (d3 - d2) - t2
    return ((n0 + n0) * t_low + n2 * t_high) * pl.reciprocal(den, approx=True)


def face(p, m):
    dp = [p[i + 1] - p[i] for i in range(4)]
    dm = [m[i + 1] - m[i] for i in range(4)]
    cp = correction(dp[0], dp[1], dp[2], dp[3])
    cm = correction(dm[3], dm[2], dm[1], dm[0])
    lin = 5.0 * (p[2] + m[2]) + 2.0 * (p[3] + m[1]) - (p[1] + m[3])
    return lin - (cp - cm)


def kernel(sizes, mag, ele, mag_out, ele_out, u, pa, pb, ra, rb, te, tr, fr, acc, vr, vt, gb, pd,
           ca, cs, crp, crm, cth, send, recv, local):
    n_row, n_theta, n_phi, nr, nt, L, plane = sizes
    row, th, ph = lax.axis_index("row"), lax.axis_index("theta"), lax.axis_index("phi")
    slot = L // nr
    halves = nt // 8
    spacing = math.pi / (nt * n_theta)
    spacing_phi = 2.0 * math.pi / (L * n_phi)
    dt = courant / (1.0 / spacing + 1.0 / spacing + 1.0 / spacing_phi)
    scale = -dt / 12.0
    planes = nr + 2 * G
    flat = u.reshape(u.shape[0], 6, (planes + 2) * plane, L)
    first, last = th == 0, th == n_theta - 1
    opposite = (row, th, lax.rem(ph + n_phi // 2, n_phi))
    right = (row, th, lax.rem(ph + 1, n_phi))
    left = (row, th, lax.rem(ph + n_phi - 1, n_phi))
    above = tuple(jnp.where(last, o, q) for o, q in zip(opposite, (row, th + 1, ph)))
    below = tuple(jnp.where(first, o, q) for o, q in zip(opposite, (row, th - 1, ph)))
    outer, inner = (row + 1, th, ph), (row - 1, th, ph)
    has_outer, has_inner = row < n_row - 1, row > 0

    loads = [
        pltpu.make_async_copy(src, u.at[0, 3 * i : 3 * i + 3, 1 + G : 1 + G + nr, 0:nt], local.at[i])
        for i, src in enumerate((mag, ele))
    ]
    for c in loads:
        c.start()

    barrier = pltpu.get_barrier_semaphore()
    for target in (above, below, right, left):
        pl.semaphore_signal(barrier, inc=1, device_id=target, device_id_type=MESH)

    @pl.when(has_outer)
    def _():
        pl.semaphore_signal(barrier, inc=1, device_id=outer, device_id_type=MESH)

    @pl.when(has_inner)
    def _():
        pl.semaphore_signal(barrier, inc=1, device_id=inner, device_id_type=MESH)

    lane = lax.broadcasted_iota(jnp.int32, (8, L), 1)
    sub = lax.broadcasted_iota(jnp.int32, (8, L), 0)
    owner = jnp.zeros((8, L), jnp.int32)
    for q in range(1, nr):
        owner = owner + (lane >= slot * q).astype(jnp.int32)
    in_slot = lane - slot * owner

    def radius_at(index):
        return inner_radius + (index.astype(jnp.float32) + 0.5) * spacing

    def lapse_shift(radius):
        ratio = 2.0 * hole_mass / radius
        return 1.0 / jnp.sqrt(1.0 + ratio), ratio / (1.0 + ratio)

    for q in range(ca.shape[0] // 8):
        a, s = lapse_shift(radius_at(row * nr - G + 8 * q + sub))
        ca[8 * q : 8 * q + 8] = a
        cs[8 * q : 8 * q + 8] = s
    for q in range(crp.shape[0] // 8):
        index = row * nr + 8 * q + sub
        rc, hi, lo = radius_at(index), radius_at(index + 1), radius_at(index - 1)
        crp[8 * q : 8 * q + 8] = scale * (0.5 * (rc + hi)) ** 2 / (rc * rc * spacing)
        crm[8 * q : 8 * q + 8] = scale * (0.5 * (rc + lo)) ** 2 / (rc * rc * spacing)
    for q in range(halves):
        index = (th * nt + 8 * q + sub).astype(jnp.float32)
        mid = jnp.sin((index + 0.5) * spacing)
        cth[0, 8 * q : 8 * q + 8] = scale * jnp.sin((index + 1.0) * spacing) / (mid * spacing)
        cth[1, 8 * q : 8 * q + 8] = scale * jnp.sin(index * spacing) / (mid * spacing)
    a_lane, s_lane = lapse_shift(radius_at(row * nr + owner))
    coef_phi = scale / spacing_phi

    zeros = jnp.zeros((nt, L), jnp.float32)
    for stage in range(3):
        @pl.when(row == 0)
        def _():
            for c in range(6):
                for q in range(G):
                    u[stage, c, 1 + q, 0:nt] = zeros

        @pl.when(row == n_row - 1)
        def _():
            for c in range(6):
                for q in range(G):
                    u[stage, c, 1 + G + nr + q, 0:nt] = zeros

    def pack(stage, r, tiles):
        mask = (lane >= slot * r) & (lane < slot * r + slot)
        for c in range(6):
            for t in range(halves):
                x = tiles[c][t]
                pa[stage, c, t] = jnp.where(mask, pltpu.roll(x, slot * r + 3, 1), pa[stage, c, t])
                pb[stage, c, t] = jnp.where(
                    mask, pltpu.roll(x, lax.rem(slot * r + 6, L), 1), pb[stage, c, t]
                )

    def tile(stage, c, r, t):
        return u[stage, c, 1 + G + r, 8 * t : 8 * t + 8]

    def remote(src, dst, stage, m_send, m_recv, target):
        return pltpu.make_async_remote_copy(
            src_ref=src, dst_ref=dst, send_sem=send.at[stage, m_send], recv_sem=recv.at[stage, m_recv],
            device_id=target, device_id_type=MESH,
        )

    base = 1 + G

    def radial_out(stage):
        return remote(u.at[stage, :, base + nr - G : base + nr, 0:nt], u.at[stage, :, 1 : 1 + G, 0:nt],
                      stage, 0, 0, outer)

    def radial_in(stage):
        return remote(u.at[stage, :, base : base + G, 0:nt],
                      u.at[stage, :, base + nr : base + nr + G, 0:nt], stage, 1, 1, inner)

    def theta_copies(stage):
        up = jnp.where(last, 1, 0)
        down = jnp.where(first, 0, 1)
        return (
            remote(te.at[stage, 1], tr.at[stage, up], stage, 2, 2 + up, above),
            remote(te.at[stage, 0], tr.at[stage, down], stage, 3, 2 + down, below),
        )

    def phi_copies(stage):
        return (
            remote(pa.at[stage], ra.at[stage], stage, 4, 4, right),
            remote(pb.at[stage], rb.at[stage], stage, 5, 5, left),
        )

    starts = list(range(0, nr - 7, 8))
    if starts[-1] + 8 < nr:
        starts.append(nr - 8)

    def grab(stage, c, r0, k):
        return flat[stage, c, pl.ds((base + r0) * plane + k, 8, stride=plane), :]

    def send_all(stage):
        @pl.when(has_outer)
        def _():
            radial_out(stage).start()

        @pl.when(has_inner)
        def _():
            radial_in(stage).start()

        for side in range(2):
            for c in range(6):
                for k in range(G):
                    for r0 in starts:
                        te[stage, side, pl.ds((c * G + k) * nr + r0, 8), :] = grab(
                            stage, c, r0, k if side == 0 else nt - G + k
                        )
        for c in theta_copies(stage) + phi_copies(stage):
            c.start()

    for c in loads:
        c.wait()

    def pack_first(r, carry):
        pack(0, r, [[tile(0, c, r, t) for t in range(halves)] for c in range(6)])
        return carry

    lax.fori_loop(0, nr, pack_first, 0)
    pl.semaphore_wait(barrier, 4 + jnp.where(has_outer, 1, 0) + jnp.where(has_inner, 1, 0))
    send_all(0)

    def rolled(v, k):
        return v if k == 0 else pltpu.roll(v, (-k) % L, 1)

    def phi_div(split_values):
        out = []
        for c, (vp, vm) in enumerate(split_values):
            p = [rolled(vp, k) for k in range(-2, 3)]
            if c in ZERO[2]:
                m = [-x for x in p[1:]] + [rolled(vm, 3)]
            else:
                m = [rolled(vm, k) for k in range(-1, 4)]
            f = face(p, m)
            out.append(coef_phi * (f - pltpu.roll(f, 1, 1)))
        return out

    def coefs(p):
        return (
            jnp.broadcast_to(ca[pl.ds(p, 1), :], (8, L)),
            jnp.broadcast_to(cs[pl.ds(p, 1), :], (8, L)),
        )

    def stage_body(stage, carry):
        def phi_pass(r, carry):
            a, s = coefs(r + G)
            for t in range(halves):
                x = [tile(stage, c, r, t) for c in range(6)]
                for c, d in enumerate(phi_div(split(2, x, a, s))):
                    acc[c, r, 8 * t : 8 * t + 8] = d
                for c, (vp, vm) in enumerate(split(0, x, a, s)):
                    vr[0, c, r + G, 8 * t : 8 * t + 8] = vp
                    vr[1, c, r + G, 8 * t : 8 * t + 8] = vm
            return carry

        lax.fori_loop(0, nr, phi_pass, 0)

        def radial_face(f, carry):
            for c in range(6):
                for t in range(halves):
                    rows = slice(8 * t, 8 * t + 8)
                    p = [vr[0, c, f + k, rows] for k in range(5)]
                    m = [vr[1, c, f + k, rows] for k in range(1, 6)]
                    fr[c, f, rows] = face(p, m)
            return carry

        lax.fori_loop(G, nr - G + 1, radial_face, 0)

        @pl.when(has_inner)
        def _():
            radial_out(stage).wait_recv()

        @pl.when(has_outer)
        def _():
            radial_in(stage).wait_recv()

        def ghost_planes(q, carry):
            p = jnp.where(q < G, q, q + nr)
            a, s = coefs(p)
            for t in range(halves):
                x = [u[stage, c, 1 + p, 8 * t : 8 * t + 8] for c in range(6)]
                for c, (vp, vm) in enumerate(split(0, x, a, s)):
                    vr[0, c, p, 8 * t : 8 * t + 8] = vp
                    vr[1, c, p, 8 * t : 8 * t + 8] = vm
            return carry

        lax.fori_loop(0, 2 * G, ghost_planes, 0)

        def outer_faces(q, carry):
            return radial_face(jnp.where(q < G, q, q + nr + 1 - 2 * G), carry)

        lax.fori_loop(0, 2 * G, outer_faces, 0)

        for side in range(2):
            remote(te.at[stage, side], tr.at[stage, side], stage, 2, 2 + side, above).wait_recv()
            pole = first if side == 0 else last
            sign = jnp.where(pole, -1.0, 1.0)
            for g in range(G):
                k = jnp.where(pole, G - 1 - g, g)
                for c in range(6):
                    for r0 in starts:
                        x = tr[stage, side, pl.ds((c * G + k) * nr + r0, 8), :]
                        if c % 3:
                            x = x * sign
                        target = (base + r0) * plane + (g - G if side == 0 else nt + g)
                        flat[stage, c, pl.ds(target, 8, stride=plane), :] = x

        for r0 in starts:
            a, s = ca[G + r0 : G + r0 + 8], cs[G + r0 : G + r0 + 8]
            v = [split(1, [grab(stage, c, r0, k) for c in range(6)], a, s) for k in range(-3, 3)]
            for c in range(6):
                gb[c, r0 : r0 + 8] = face([v[k][c][0] for k in range(5)], [v[k][c][1] for k in range(1, 6)])

        for c in phi_copies(stage):
            c.wait_recv()

        def packed(t, carry):
            xa = [jnp.where(in_slot < 3, ra[stage, c, t], pa[stage, c, t]) for c in range(6)]
            xb = [jnp.where(in_slot >= 6, rb[stage, c, t], pb[stage, c, t]) for c in range(6)]
            da = phi_div(split(2, xa, a_lane, s_lane))
            db = phi_div(split(2, xb, a_lane, s_lane))
            for c in range(6):
                pd[c, t] = jnp.where(in_slot < 6, db[c], pltpu.roll(da[c], 3, 1))
            return carry

        lax.fori_loop(0, halves, packed, 0)

        w = jnp.where(stage == 0, 0.0, jnp.where(stage == 1, 0.75, 1.0 / 3.0)).astype(jnp.float32)
        edge = (lane < 3) | (lane >= L - 3)

        def final(r, carry):
            a, s = coefs(r + G)
            top = (base + r) * plane - G
            for q in range(halves + 1):
                x = [flat[stage, c, pl.ds(top + 8 * q, 8), :] for c in range(6)]
                for c, (vp, vm) in enumerate(split(1, x, a, s)):
                    vt[0, c, 8 * q : 8 * q + 8] = vp
                    vt[1, c, 8 * q : 8 * q + 8] = vm
            rp = jnp.broadcast_to(crp[pl.ds(r, 1), :], (8, L))
            rm = jnp.broadcast_to(crm[pl.ds(r, 1), :], (8, L))
            new = [[None] * halves for _ in range(6)]
            for c in range(6):
                before = jnp.broadcast_to(gb[c, pl.ds(r, 1), :], (8, L))
                for t in range(halves):
                    rows = slice(8 * t, 8 * t + 8)
                    f = face([vt[0, c, 8 * t + k : 8 * t + k + 8] for k in range(1, 6)],
                             [vt[1, c, 8 * t + k : 8 * t + k + 8] for k in range(2, 7)])
                    turned = pltpu.roll(f, 1, 0)
                    lower = jnp.where(sub == 0, before, turned)
                    before = turned
                    patch = pltpu.roll(pd[c, t], lax.rem(L + L - 6 - slot * r, L), 1)
                    rate = jnp.where(edge, patch, acc[c, r, rows])
                    rate = rate + (cth[0, rows] * f - cth[1, rows] * lower)
                    rate = rate + (rp * fr[c, r + 1, rows] - rm * fr[c, r, rows])
                    new[c][t] = w * tile(0, c, r, t) + (1.0 - w) * (tile(stage, c, r, t) + rate)
            for t in range(halves):
                b, d = [new[c][t] for c in range(3)], [new[c][t] for c in range(3, 6)]
                b2 = jnp.maximum(b[0] * b[0] + b[1] * b[1] + b[2] * b[2], 1.0)
                along = (b[0] * d[0] + b[1] * d[1] + b[2] * d[2]) / b2
                d = [y - along * x for x, y in zip(b, d)]
                d2 = d[0] * d[0] + d[1] * d[1] + d[2] * d[2]
                shrink = jnp.sqrt(b2 / jnp.maximum(d2, b2))
                for c in range(3):
                    new[3 + c][t] = d[c] * shrink
                for c in range(6):
                    u[stage + 1, c, base + r, 8 * t : 8 * t + 8] = new[c][t]

            @pl.when(stage < 2)
            def _():
                pack(stage + 1, r, new)

            return carry

        lax.fori_loop(0, nr, final, 0)

        @pl.when(stage < 2)
        def _():
            send_all(stage + 1)

        return carry

    lax.fori_loop(0, 3, stage_body, 0)
    stores = [
        pltpu.make_async_copy(u.at[3, 3 * i : 3 * i + 3, base : base + nr, 0:nt], dst, local.at[i])
        for i, dst in enumerate((mag_out, ele_out))
    ]
    for c in stores:
        c.start()

    def drain(stage, carry):
        @pl.when(has_outer)
        def _():
            radial_out(stage).wait_send()

        @pl.when(has_inner)
        def _():
            radial_in(stage).wait_send()

        for c in theta_copies(stage) + phi_copies(stage):
            c.wait_send()
        return carry

    lax.fori_loop(0, 3, drain, 0)
    for c in stores:
        c.wait()


def solution(mesh):
    n_row, n_theta, n_phi = (mesh.shape[k] for k in ("row", "theta", "phi"))

    def body(magnetic, electric):
        _, nr, nt, lanes = magnetic.shape
        plane = -(-(nt + 2 * G) // 8) * 8
        planes = nr + 2 * G
        halves = nt // 8
        pad8 = lambda n: -(-n // 8) * 8
        f32 = jnp.float32
        vm = lambda *shape: pltpu.VMEM(shape, f32)
        sizes = (n_row, n_theta, n_phi, nr, nt, lanes, plane)
        anywhere = pl.BlockSpec(memory_space=pl.ANY)
        packs = vm(3, 6, halves, 8, lanes)
        return pl.pallas_call(
            functools.partial(kernel, sizes),
            out_shape=[jax.ShapeDtypeStruct(magnetic.shape, f32)] * 2,
            in_specs=[anywhere] * 2,
            out_specs=[anywhere] * 2,
            scratch_shapes=[
                vm(4, 6, planes + 2, plane, lanes),
                packs, packs, packs, packs,
                vm(3, 2, 6 * G * nr, lanes),
                vm(3, 2, 6 * G * nr, lanes),
                vm(6, nr + 1, nt, lanes),
                vm(6, nr, nt, lanes),
                vm(2, 6, planes, nt, lanes),
                vm(2, 6, nt + 8, lanes),
                vm(6, pad8(nr), lanes),
                vm(6, halves, 8, lanes),
                vm(pad8(planes), lanes),
                vm(pad8(planes), lanes),
                vm(pad8(nr), lanes),
                vm(pad8(nr), lanes),
                vm(2, nt, lanes),
                pltpu.SemaphoreType.DMA((3, 6)),
                pltpu.SemaphoreType.DMA((3, 6)),
                pltpu.SemaphoreType.DMA((2,)),
            ],
            compiler_params=pltpu.CompilerParams(collective_id=0, has_side_effects=True),
        )(magnetic, electric)

    spec = P(None, "row", "theta", "phi")
    return jax.shard_map(body, mesh=mesh, in_specs=(spec, spec), out_specs=(spec, spec), check_vma=False)
```

time: 318 us -> 39.9 us (0.13); the launches traced: 313 us -> 39.7 us
  other arithmetic: 162 us -> 0 us
  local copies, waits for them, and re-layouts: 64.2 us -> 2.46 us
  starting transfers between devices: 43.8 us -> 0 us
  waiting for transfers between devices: 41.1 us -> 0 us
  Pallas kernels: 0 us -> 36.6 us
    dynamic_update_slice x54 -> x0, other arithmetic: 67.4 us -> none  [face_fluxes(): lax.map(lambda couple: interface(couple[0], couple[1], axis), (fluxes, fi...]
    mul x55 -> x0, other arithmetic: 53.5 us -> none  [the longest x54 53.5 us: interface(): plus_part = 0.5 * (flux + wave_speed * field)]
    ppermute x21 -> x0, starting transfers between devices: 43.8 us -> none  [the longest x9 29.9 us: padded_2(): lax.ppermute(lax.slice_in_dim(block, block.shape[dim] - width, None, axis...]
    ppermute x21 -> x0, waiting for transfers between devices: 41.1 us -> none  [the longest x3 18.6 us: from_behind(): lax.ppermute(array, axis, [(i, (i + by) % length) for i in range(length)])]
    pallas_call x0 -> x1, Pallas kernels: none -> 36.6 us  [body(): pl.pallas_call(functools.partial(kernel, sizes), out_shape=[jax.ShapeDtyp...]
    slice x23 -> x0, local copies, waits for them, and re-layouts: 29 us -> none  [the longest x3 8.21 us: tendency(): polar_flux[:, 3:-3, :, 3:-3]]
    unnamed x94 -> x4, local copies, waits for them, and re-layouts: 20.4 us -> 2.46 us
    select_n x9 -> x0, other arithmetic: 10.1 us -> none  [the longest x3 5.88 us: body(): outgoing = jnp.where(theta_index == 0, north_rows, south_rows)]
  transfers between devices with their start and end apart: 21 -> 0, of which waited for: 14 -> 0; matrix products, arithmetic and copies ran while one was open for 6% -> 0% of each run, Pallas kernels for 0% -> 0%
where the time goes in v1:
time: 39.9 us; the launch traced here: 39.7 us
  Pallas kernels  36.6 us (92%)
  local copies, waits for them, and re-layouts  2.46 us (6%)
  between operations  0.65 us (2%)
    pallas_call x1, Pallas kernels, body(): pl.pallas_call(functools.partial(kernel, sizes), out_shape=[jax.ShapeDtyp...  36.6 us
    unnamed x4, local copies, waits for them, and re-layouts  2.46 us

profile of v1, /device:TPU:0, one launch (start us, length us, event | category | flops | bytes accessed | tf_op | source)
XLA Modules:
  0.0 39.7 jit_solution(15079250686733189899)
XLA Ops:
  0.6 36.6 %shard_map.41 = (f32[3,12,16,128]{3,2,1,0:T(8,128)}, f32[3,12,16,128]{3,2,1,0:T(8,128)}) custom-call(f32[3,12,16,128]{3,2,1,0:T(8,128)} %mag.1, f32[3,12,16,128]{3,2,1,0:T(8,128)} %ele.1), custom_call_target="tpu_custom_call" | custom-call | tf_op jit(solution)/shard_map/pallas_call | solution.py:435
  37.3 0.0 copy-start
  37.3 1.7 %copy.6 = f32[3,12,16,128]{3,2,1,0:T(8,128)} copy(f32[3,12,16,128]{3,2,1,0:T(8,128)} %get-tuple-element.4) | data formatting | bytes 589824
  39.0 0.0 copy-done
  39.0 0.7 %copy.7 = f32[3,12,16,128]{3,2,1,0:T(8,128)} copy(f32[3,12,16,128]{3,2,1,0:T(8,128)S(1)} %copy-done) | data formatting | bytes 589824
Async XLA Ops:
  37.3 1.8 %copy-start = (f32[3,12,16,128]{3,2,1,0:T(8,128)S(1)}, f32[3,12,16,128]{3,2,1,0:T(8,128)}, u32[]{:S(2)}) copy-start(f32[3,12,16,128]{3,2,1,0:T(8,128)} %get-tuple-element.5) | copy-start | bytes 884740

commit v2 on v1

--- a/solution.py
+++ b/solution.py
@@ -41,34 +41,67 @@
     return out
 
 
-def correction(d0, d1, d2, d3):
-    k, eps = 0.609375, 3.0 * smooth_eps
-    r1 = (k * d1) * d1 + eps
-    r2 = (k * d2) * d2 + eps
-    x0 = d0 - 1.375 * d1
-    x1 = d1 - 0.625 * d2
-    x2 = d3 - 1.375 * d2
-    s0, s1, s2 = x0 * x0 + r1, x1 * x1 + r2, x2 * x2 + r2
+class Line:
+    def __init__(self, d, r=None, t3=None):
+        self.made, self.d0, self.r0, self.t0 = {}, d, r, t3
+
+    def keep(self, kind, i, make):
+        if (kind, i) not in self.made:
+            self.made[kind, i] = make()
+        return self.made[kind, i]
+
+    def d(self, i):
+        return self.keep(0, i, lambda: self.d0(i))
+
+    def square(self, i):
+        k, eps = 0.609375, 3.0 * smooth_eps
+        return (k * self.d(i)) * self.d(i) + eps
+
+    def r(self, i):
+        return self.keep(1, i, lambda: self.r0(i) if self.r0 else self.square(i))
+
+    def q(self, i):
+        return self.keep(2, i, lambda: 1.375 * self.d(i))
+
+    def h(self, i):
+        return self.keep(3, i, lambda: 0.625 * self.d(i))
+
+    def step(self, i):
+        return self.keep(4, i, lambda: self.d(i) - self.d(i - 1))
+
+    def third(self, i):
+        return self.step(i + 1) - self.step(i)
+
+    def t(self, i):
+        return self.keep(5, i, lambda: self.t0(i) if self.t0 else self.third(i))
+
+
+def correction(line, i, way):
+    i0, i1, i3 = i - 2 * way, i - way, i + way
+    x0 = line.d(i0) - line.q(i1)
+    x1 = line.d(i1) - line.h(i)
+    x2 = line.d(i3) - line.q(i)
+    s0, s1, s2 = x0 * x0 + line.r(i1), x1 * x1 + line.r(i), x2 * x2 + line.r(i)
     s0, s1, s2 = s0 * s0, s1 * s1, s2 * s2
     z = 3.0 * s0
     n0, n2, y = s1 * s2, z * s1, z * s2
     den = (n0 + n2) + (y + y)
-    t2 = d2 - d1
-    t_low = t2 - (d1 - d0)
-    t_high = (d3 - d2) - t2
-    return ((n0 + n0) * t_low + n2 * t_high) * pl.reciprocal(den, approx=True)
-
-
-def face(p, m):
-    dp = [p[i + 1] - p[i] for i in range(4)]
-    dm = [m[i + 1] - m[i] for i in range(4)]
-    cp = correction(dp[0], dp[1], dp[2], dp[3])
-    cm = correction(dm[3], dm[2], dm[1], dm[0])
-    lin = 5.0 * (p[2] + m[2]) + 2.0 * (p[3] + m[1]) - (p[1] + m[3])
-    return lin - (cp - cm)
-
-
-def kernel(sizes, mag, ele, mag_out, ele_out, u, pa, pb, ra, rb, te, tr, fr, acc, vr, vt, gb, pd,
+    return ((n0 + n0) * line.t(i1) + n2 * line.t(i)) * pl.reciprocal(den, approx=True)
+
+
+def face(p, m, double, i=0):
+    if m is None:
+        return p.t(i) - (correction(p, i, 1) + correction(p, i, -1))
+    dm = m.d(i)
+    lin = 6.0 * double + ((p.d(i - 1) - m.d(i + 1)) + 2.0 * (p.d(i) + (dm + dm)))
+    return lin - (correction(p, i, 1) - correction(m, i, -1))
+
+
+def line_of(values, start=0):
+    return Line(lambda i: values[i + 1 - start] - values[i - start])
+
+
+def kernel(sizes, mag, ele, mag_out, ele_out, u, pa, pb, sa, sb, ra, rb, te, tr, fr, acc, vr, vt, vd, vs, gb, pd,
            ca, cs, crp, crm, cth, send, recv, local):
     n_row, n_theta, n_phi, nr, nt, L, plane = sizes
     row, th, ph = lax.axis_index("row"), lax.axis_index("theta"), lax.axis_index("phi")
@@ -192,8 +225,8 @@
 
     def phi_copies(stage):
         return (
-            remote(pa.at[stage], ra.at[stage], stage, 4, 4, right),
-            remote(pb.at[stage], rb.at[stage], stage, 5, 5, left),
+            remote(sa.at[stage], ra.at[stage], stage, 4, 4, right),
+            remote(sb.at[stage], rb.at[stage], stage, 5, 5, left),
         )
 
     starts = list(range(0, nr - 7, 8))
@@ -212,6 +245,14 @@
         def _():
             radial_in(stage).start()
 
+        for g in range(2):
+            for t in range(halves):
+                x, y = pa[stage, 3 * g + 1, t], pa[stage, 3 * g + 2, t]
+                x = jnp.where(in_slot < 6, pltpu.roll(x, 3, 1), pltpu.roll(y, 6, 1))
+                sa[stage, g, t] = jnp.where(in_slot < 3, pa[stage, 3 * g, t], x)
+                x, y = pb[stage, 3 * g + 1, t], pb[stage, 3 * g + 2, t]
+                x = jnp.where(in_slot < 3, pltpu.roll(y, L - 6, 1), pltpu.roll(x, L - 3, 1))
+                sb[stage, g, t] = jnp.where(in_slot < 6, x, pb[stage, 3 * g, t])
         for side in range(2):
             for c in range(6):
                 for k in range(G):
@@ -236,15 +277,27 @@
     def rolled(v, k):
         return v if k == 0 else pltpu.roll(v, (-k) % L, 1)
 
+    def turning(v):
+        made = {}
+
+        def at(kind, i, make):
+            if i == 0:
+                if kind not in made:
+                    made[kind] = make()
+                return made[kind]
+            return rolled(at(kind, 0, make), i)
+
+        line = Line(
+            lambda i: at(0, i, lambda: rolled(v, 1) - v),
+            lambda i: at(1, i, lambda: line.square(0)),
+            lambda i: at(2, i, lambda: line.third(0)),
+        )
+        return line
+
     def phi_div(split_values):
         out = []
         for c, (vp, vm) in enumerate(split_values):
-            p = [rolled(vp, k) for k in range(-2, 3)]
-            if c in ZERO[2]:
-                m = [-x for x in p[1:]] + [rolled(vm, 3)]
-            else:
-                m = [rolled(vm, k) for k in range(-1, 4)]
-            f = face(p, m)
+            f = face(turning(vp), None if c in ZERO[2] else turning(vm), vp + vm)
             out.append(coef_phi * (f - pltpu.roll(f, 1, 1)))
         return out
 
@@ -268,16 +321,24 @@
 
         lax.fori_loop(0, nr, phi_pass, 0)
 
-        def radial_face(f, carry):
-            for c in range(6):
-                for t in range(halves):
-                    rows = slice(8 * t, 8 * t + 8)
-                    p = [vr[0, c, f + k, rows] for k in range(5)]
-                    m = [vr[1, c, f + k, rows] for k in range(1, 6)]
-                    fr[c, f, rows] = face(p, m)
-            return carry
-
-        lax.fori_loop(G, nr - G + 1, radial_face, 0)
+        def radial_faces(lo, hi):
+            def part(t, carry):
+                rows = pl.ds(pl.multiple_of(8 * t, 8), 8)
+                for c in range(6):
+                    p = [vr[0, c, k, rows] for k in range(lo, hi + 5)]
+                    pline, mline, m = line_of(p, lo), None, None
+                    if c not in ZERO[0]:
+                        m = [vr[1, c, k, rows] for k in range(lo, hi + 5)]
+                        mline = line_of(m, lo)
+                    for f in range(lo, hi):
+                        i = f + 2
+                        double = None if m is None else p[i - lo] + m[i - lo]
+                        fr[c, f, rows] = face(pline, mline, double, i)
+                return carry
+
+            lax.fori_loop(0, halves, part, 0)
+
+        radial_faces(G, nr - G + 1)
 
         @pl.when(has_inner)
         def _():
@@ -299,10 +360,8 @@
 
         lax.fori_loop(0, 2 * G, ghost_planes, 0)
 
-        def outer_faces(q, carry):
-            return radial_face(jnp.where(q < G, q, q + nr + 1 - 2 * G), carry)
-
-        lax.fori_loop(0, 2 * G, outer_faces, 0)
+        radial_faces(0, G)
+        radial_faces(nr - G + 1, nr + 1)
 
         for side in range(2):
             remote(te.at[stage, side], tr.at[stage, side], stage, 2, 2 + side, above).wait_recv()
@@ -322,14 +381,22 @@
             a, s = ca[G + r0 : G + r0 + 8], cs[G + r0 : G + r0 + 8]
             v = [split(1, [grab(stage, c, r0, k) for c in range(6)], a, s) for k in range(-3, 3)]
             for c in range(6):
-                gb[c, r0 : r0 + 8] = face([v[k][c][0] for k in range(5)], [v[k][c][1] for k in range(1, 6)])
+                pline = line_of([v[k][c][0] for k in range(6)], -2)
+                mline = None if c in ZERO[1] else line_of([v[k][c][1] for k in range(6)], -2)
+                gb[c, r0 : r0 + 8] = face(pline, mline, v[2][c][0] + v[2][c][1])
 
         for c in phi_copies(stage):
             c.wait_recv()
 
         def packed(t, carry):
-            xa = [jnp.where(in_slot < 3, ra[stage, c, t], pa[stage, c, t]) for c in range(6)]
-            xb = [jnp.where(in_slot >= 6, rb[stage, c, t], pb[stage, c, t]) for c in range(6)]
+            xa = [
+                jnp.where(in_slot < 3, rolled(ra[stage, c // 3, t], 3 * (c % 3)), pa[stage, c, t])
+                for c in range(6)
+            ]
+            xb = [
+                jnp.where(in_slot >= 6, rolled(rb[stage, c // 3, t], -3 * (c % 3)), pb[stage, c, t])
+                for c in range(6)
+            ]
             da = phi_div(split(2, xa, a_lane, s_lane))
             db = phi_div(split(2, xb, a_lane, s_lane))
             for c in range(6):
@@ -346,9 +413,15 @@
             top = (base + r) * plane - G
             for q in range(halves + 1):
                 x = [flat[stage, c, pl.ds(top + 8 * q, 8), :] for c in range(6)]
-                for c, (vp, vm) in enumerate(split(1, x, a, s)):
-                    vt[0, c, 8 * q : 8 * q + 8] = vp
-                    vt[1, c, 8 * q : 8 * q + 8] = vm
+                for c, values in enumerate(split(1, x, a, s)):
+                    for sign, v in enumerate(values):
+                        vt[sign, c, 8 * q : 8 * q + 8] = v
+            for c in range(6):
+                for sign in range(1 if c in ZERO[1] else 2):
+                    for q in range(halves + 1):
+                        d = vt[sign, c, 8 * q + 1 : 8 * q + 9] - vt[sign, c, 8 * q : 8 * q + 8]
+                        vd[sign, c, 8 * q : 8 * q + 8] = d
+                        vs[sign, c, 8 * q : 8 * q + 8] = Line(lambda i: d).square(0)
             rp = jnp.broadcast_to(crp[pl.ds(r, 1), :], (8, L))
             rm = jnp.broadcast_to(crm[pl.ds(r, 1), :], (8, L))
             new = [[None] * halves for _ in range(6)]
@@ -356,8 +429,14 @@
                 before = jnp.broadcast_to(gb[c, pl.ds(r, 1), :], (8, L))
                 for t in range(halves):
                     rows = slice(8 * t, 8 * t + 8)
-                    f = face([vt[0, c, 8 * t + k : 8 * t + k + 8] for k in range(1, 6)],
-                             [vt[1, c, 8 * t + k : 8 * t + k + 8] for k in range(2, 7)])
+                    lines = [
+                        Line(lambda i, g=g: vd[g, c, 8 * t + 3 + i : 8 * t + 11 + i],
+                             lambda i, g=g: vs[g, c, 8 * t + 3 + i : 8 * t + 11 + i])
+                        for g in range(1 if c in ZERO[1] else 2)
+                    ]
+                    here = slice(8 * t + 3, 8 * t + 11)
+                    double = None if c in ZERO[1] else vt[0, c, here] + vt[1, c, here]
+                    f = face(lines[0], lines[1] if len(lines) > 1 else None, double)
                     turned = pltpu.roll(f, 1, 0)
                     lower = jnp.where(sub == 0, before, turned)
                     before = turned
@@ -432,6 +511,7 @@
         sizes = (n_row, n_theta, n_phi, nr, nt, lanes, plane)
         anywhere = pl.BlockSpec(memory_space=pl.ANY)
         packs = vm(3, 6, halves, 8, lanes)
+        joined = vm(3, 2, halves, 8, lanes)
         return pl.pallas_call(
             functools.partial(kernel, sizes),
             out_shape=[jax.ShapeDtypeStruct(magnetic.shape, f32)] * 2,
@@ -439,13 +519,16 @@
             out_specs=[anywhere] * 2,
             scratch_shapes=[
                 vm(4, 6, planes + 2, plane, lanes),
-                packs, packs, packs, packs,
+                packs, packs,
+                joined, joined, joined, joined,
                 vm(3, 2, 6 * G * nr, lanes),
                 vm(3, 2, 6 * G * nr, lanes),
                 vm(6, nr + 1, nt, lanes),
                 vm(6, nr, nt, lanes),
                 vm(2, 6, planes, nt, lanes),
-                vm(2, 6, nt + 8, lanes),
+                vm(2, 6, nt + 16, lanes),
+                vm(2, 6, nt + 16, lanes),
+                vm(2, 6, nt + 16, lanes),
                 vm(6, pad8(nr), lanes),
                 vm(6, halves, 8, lanes),
                 vm(pad8(planes), lanes),
@@ -457,7 +540,9 @@
                 pltpu.SemaphoreType.DMA((3, 6)),
                 pltpu.SemaphoreType.DMA((2,)),
             ],
-            compiler_params=pltpu.CompilerParams(collective_id=0, has_side_effects=True),
+            compiler_params=pltpu.CompilerParams(
+                collective_id=0, has_side_effects=True, vmem_limit_bytes=24 * 1024 * 1024
+            ),
         )(magnetic, electric)
 
     spec = P(None, "row", "theta", "phi")

time: 39.9 us -> 39.7 us (level)
  Pallas kernels: 36.6 us -> 35.6 us
  local copies, waits for them, and re-layouts: 2.46 us -> 3.35 us
    pallas_call x1, Pallas kernels: 36.6 us -> 35.6 us  [body(): pl.pallas_call(functools.partial(kernel, sizes), out_shape=[jax.ShapeDtyp...]
    unnamed x4 -> x6, local copies, waits for them, and re-layouts: 2.46 us -> 3.35 us
where the time goes in v2:
time: 39.7 us; the launch traced here: 39.6 us
  Pallas kernels  35.6 us (90%)
  local copies, waits for them, and re-layouts  3.35 us (8%)
  between operations  0.65 us (2%)
    pallas_call x1, Pallas kernels, body(): pl.pallas_call(functools.partial(kernel, sizes), out_shape=[jax.ShapeDtyp...  35.6 us
    unnamed x6, local copies, waits for them, and re-layouts  3.35 us

profile of v2, /device:TPU:0, one launch (start us, length us, event | category | flops | bytes accessed | tf_op | source)
XLA Modules:
  0.0 39.6 jit_solution(4050203510258422042)
XLA Ops:
  0.6 0.0 copy-start
  0.6 1.0 %copy-done = f32[3,12,16,128]{3,2,1,0:T(8,128)S(1)} copy-done((f32[3,12,16,128]{3,2,1,0:T(8,128)S(1)}, f32[3,12,16,128]{3,2,1,0:T(8,128)}, u32[]{:S(2)}) %copy-start) | copy-done | bytes 294936
  1.6 0.0 copy-start.1
  1.6 1.0 %copy-done.1 = f32[3,12,16,128]{3,2,1,0:T(8,128)S(1)} copy-done((f32[3,12,16,128]{3,2,1,0:T(8,128)S(1)}, f32[3,12,16,128]{3,2,1,0:T(8,128)}, u32[]{:S(2)}) %copy-start.1) | copy-done | bytes 294936
  2.6 35.6 %shard_map.41 = (f32[3,12,16,128]{3,2,1,0:T(8,128)S(1)}, f32[3,12,16,128]{3,2,1,0:T(8,128)S(1)}) custom-call(f32[3,12,16,128]{3,2,1,0:T(8,128)S(1)} %copy-done, f32[3,12,16,128]{3,2,1,0:T(8,128)S(1)} %copy-done.1), custom_call_target="tpu_custom_call" | custom-call | tf_op jit(solution)/shard_map/pallas_call | solution.py:515
  38.1 0.7 %copy.6 = f32[3,12,16,128]{3,2,1,0:T(8,128)} copy(f32[3,12,16,128]{3,2,1,0:T(8,128)S(1)} %get-tuple-element.4) | data formatting | bytes 589824
  38.8 0.7 %copy.7 = f32[3,12,16,128]{3,2,1,0:T(8,128)} copy(f32[3,12,16,128]{3,2,1,0:T(8,128)S(1)} %get-tuple-element.5) | data formatting | bytes 589824
Async XLA Ops:
  0.6 1.0 %copy-start = (f32[3,12,16,128]{3,2,1,0:T(8,128)S(1)}, f32[3,12,16,128]{3,2,1,0:T(8,128)}, u32[]{:S(2)}) copy-start(f32[3,12,16,128]{3,2,1,0:T(8,128)} %mag.1) | copy-start | bytes 884740
  1.6 1.0 %copy-start.1 = (f32[3,12,16,128]{3,2,1,0:T(8,128)S(1)}, f32[3,12,16,128]{3,2,1,0:T(8,128)}, u32[]{:S(2)}) copy-start(f32[3,12,16,128]{3,2,1,0:T(8,128)} %ele.1) | copy-start | bytes 884740

commit v3 on v2

--- a/solution.py
+++ b/solution.py
@@ -101,7 +101,7 @@
     return Line(lambda i: values[i + 1 - start] - values[i - start])
 
 
-def kernel(sizes, mag, ele, mag_out, ele_out, u, pa, pb, sa, sb, ra, rb, te, tr, fr, acc, vr, vt, vd, vs, gb, pd,
+def kernel(sizes, mag, ele, mag_out, ele_out, u, pa, pb, sa, sb, ra, rb, te0, te1, tr0, tr1, fr, acc, vr, vt, vd, vs, gb, pd,
            ca, cs, crp, crm, cth, send, recv, local):
     n_row, n_theta, n_phi, nr, nt, L, plane = sizes
     row, th, ph = lax.axis_index("row"), lax.axis_index("theta"), lax.axis_index("phi")
@@ -215,12 +215,14 @@
         return remote(u.at[stage, :, base : base + G, 0:nt],
                       u.at[stage, :, base + nr : base + nr + G, 0:nt], stage, 1, 1, inner)
 
-    def theta_copies(stage):
+    def theta_copies(stage, part):
         up = jnp.where(last, 1, 0)
         down = jnp.where(first, 0, 1)
+        te, tr = (te0, te1)[part], (tr0, tr1)[part]
+        n = 2 + 4 * part
         return (
-            remote(te.at[stage, 1], tr.at[stage, up], stage, 2, 2 + up, above),
-            remote(te.at[stage, 0], tr.at[stage, down], stage, 3, 2 + down, below),
+            remote(te.at[stage, 1], tr.at[stage, up], stage, n, n + up, above),
+            remote(te.at[stage, 0], tr.at[stage, down], stage, n + 1, n + down, below),
         )
 
     def phi_copies(stage):
@@ -236,7 +238,10 @@
     def grab(stage, c, r0, k):
         return flat[stage, c, pl.ds((base + r0) * plane + k, 8, stride=plane), :]
 
-    def send_all(stage):
+    def row_of(q):
+        return jnp.where(q < G, q, jnp.where(q < 2 * G, q + nr - 2 * G, q - G))
+
+    def send_radial(stage):
         @pl.when(has_outer)
         def _():
             radial_out(stage).start()
@@ -245,6 +250,22 @@
         def _():
             radial_in(stage).start()
 
+    def send_theta(stage, part):
+        te = (te0, te1)[part]
+
+        def gather(q, carry):
+            top = (base + row_of(q + 2 * G * part)) * plane
+            for side in range(2):
+                for c in range(6):
+                    x = flat[stage, c, pl.ds(top + (nt - G) * side, G), :]
+                    te[stage, side, pl.ds((q * 6 + c) * G, G), :] = x
+            return carry
+
+        lax.fori_loop(0, (2 * G, nr - 2 * G)[part], gather, 0)
+        for c in theta_copies(stage, part):
+            c.start()
+
+    def send_phi(stage):
         for g in range(2):
             for t in range(halves):
                 x, y = pa[stage, 3 * g + 1, t], pa[stage, 3 * g + 2, t]
@@ -253,26 +274,23 @@
                 x, y = pb[stage, 3 * g + 1, t], pb[stage, 3 * g + 2, t]
                 x = jnp.where(in_slot < 3, pltpu.roll(y, L - 6, 1), pltpu.roll(x, L - 3, 1))
                 sb[stage, g, t] = jnp.where(in_slot < 6, x, pb[stage, 3 * g, t])
-        for side in range(2):
-            for c in range(6):
-                for k in range(G):
-                    for r0 in starts:
-                        te[stage, side, pl.ds((c * G + k) * nr + r0, 8), :] = grab(
-                            stage, c, r0, k if side == 0 else nt - G + k
-                        )
-        for c in theta_copies(stage) + phi_copies(stage):
+        for c in phi_copies(stage):
             c.start()
 
     for c in loads:
         c.wait()
+
+    pl.semaphore_wait(barrier, 4 + jnp.where(has_outer, 1, 0) + jnp.where(has_inner, 1, 0))
+    send_radial(0)
+    for part in range(2):
+        send_theta(0, part)
 
     def pack_first(r, carry):
         pack(0, r, [[tile(0, c, r, t) for t in range(halves)] for c in range(6)])
         return carry
 
     lax.fori_loop(0, nr, pack_first, 0)
-    pl.semaphore_wait(barrier, 4 + jnp.where(has_outer, 1, 0) + jnp.where(has_inner, 1, 0))
-    send_all(0)
+    send_phi(0)
 
     def rolled(v, k):
         return v if k == 0 else pltpu.roll(v, (-k) % L, 1)
@@ -363,19 +381,26 @@
         radial_faces(0, G)
         radial_faces(nr - G + 1, nr + 1)
 
-        for side in range(2):
-            remote(te.at[stage, side], tr.at[stage, side], stage, 2, 2 + side, above).wait_recv()
-            pole = first if side == 0 else last
-            sign = jnp.where(pole, -1.0, 1.0)
-            for g in range(G):
-                k = jnp.where(pole, G - 1 - g, g)
-                for c in range(6):
-                    for r0 in starts:
-                        x = tr[stage, side, pl.ds((c * G + k) * nr + r0, 8), :]
-                        if c % 3:
-                            x = x * sign
-                        target = (base + r0) * plane + (g - G if side == 0 else nt + g)
-                        flat[stage, c, pl.ds(target, 8, stride=plane), :] = x
+        for part in range(2):
+            te, tr = (te0, te1)[part], (tr0, tr1)[part]
+            for side in range(2):
+                remote(te.at[stage, side], tr.at[stage, side], stage, 2, 2 + 4 * part + side, above).wait_recv()
+
+            def scatter(q, carry):
+                top = (base + row_of(q + 2 * G * part)) * plane
+                for side in range(2):
+                    pole = first if side == 0 else last
+                    sign = jnp.where(pole, -1.0, 1.0)
+                    for g in range(G):
+                        k = jnp.where(pole, G - 1 - g, g)
+                        for c in range(6):
+                            x = tr[stage, side, pl.ds((q * 6 + c) * G + k, 1), :]
+                            if c % 3:
+                                x = x * sign
+                            flat[stage, c, pl.ds(top + (g - G if side == 0 else nt + g), 1), :] = x
+                return carry
+
+            lax.fori_loop(0, (2 * G, nr - 2 * G)[part], scatter, 0)
 
         for r0 in starts:
             a, s = ca[G + r0 : G + r0 + 8], cs[G + r0 : G + r0 + 8]
@@ -408,20 +433,21 @@
         w = jnp.where(stage == 0, 0.0, jnp.where(stage == 1, 0.75, 1.0 / 3.0)).astype(jnp.float32)
         edge = (lane < 3) | (lane >= L - 3)
 
-        def final(r, carry):
+        def final(q, carry):
+            r = row_of(q)
             a, s = coefs(r + G)
             top = (base + r) * plane - G
-            for q in range(halves + 1):
-                x = [flat[stage, c, pl.ds(top + 8 * q, 8), :] for c in range(6)]
+            for o in range(halves + 1):
+                x = [flat[stage, c, pl.ds(top + 8 * o, 8), :] for c in range(6)]
                 for c, values in enumerate(split(1, x, a, s)):
                     for sign, v in enumerate(values):
-                        vt[sign, c, 8 * q : 8 * q + 8] = v
+                        vt[sign, c, 8 * o : 8 * o + 8] = v
             for c in range(6):
                 for sign in range(1 if c in ZERO[1] else 2):
-                    for q in range(halves + 1):
-                        d = vt[sign, c, 8 * q + 1 : 8 * q + 9] - vt[sign, c, 8 * q : 8 * q + 8]
-                        vd[sign, c, 8 * q : 8 * q + 8] = d
-                        vs[sign, c, 8 * q : 8 * q + 8] = Line(lambda i: d).square(0)
+                    for o in range(halves + 1):
+                        d = vt[sign, c, 8 * o + 1 : 8 * o + 9] - vt[sign, c, 8 * o : 8 * o + 8]
+                        vd[sign, c, 8 * o : 8 * o + 8] = d
+                        vs[sign, c, 8 * o : 8 * o + 8] = Line(lambda i: d).square(0)
             rp = jnp.broadcast_to(crp[pl.ds(r, 1), :], (8, L))
             rm = jnp.broadcast_to(crm[pl.ds(r, 1), :], (8, L))
             new = [[None] * halves for _ in range(6)]
@@ -463,11 +489,19 @@
 
             return carry
 
-        lax.fori_loop(0, nr, final, 0)
+        lax.fori_loop(0, 2 * G, final, 0)
 
         @pl.when(stage < 2)
         def _():
-            send_all(stage + 1)
+            send_radial(stage + 1)
+            send_theta(stage + 1, 0)
+
+        lax.fori_loop(2 * G, nr, final, 0)
+
+        @pl.when(stage < 2)
+        def _():
+            send_theta(stage + 1, 1)
+            send_phi(stage + 1)
 
         return carry
 
@@ -488,7 +522,7 @@
         def _():
             radial_in(stage).wait_send()
 
-        for c in theta_copies(stage) + phi_copies(stage):
+        for c in theta_copies(stage, 0) + theta_copies(stage, 1) + phi_copies(stage):
             c.wait_send()
         return carry
 
@@ -511,6 +545,7 @@
         sizes = (n_row, n_theta, n_phi, nr, nt, lanes, plane)
         anywhere = pl.BlockSpec(memory_space=pl.ANY)
         packs = vm(3, 6, halves, 8, lanes)
+        edges = lambda n: vm(3, 2, 6 * G * n, lanes)
         joined = vm(3, 2, halves, 8, lanes)
         return pl.pallas_call(
             functools.partial(kernel, sizes),
@@ -521,8 +556,8 @@
                 vm(4, 6, planes + 2, plane, lanes),
                 packs, packs,
                 joined, joined, joined, joined,
-                vm(3, 2, 6 * G * nr, lanes),
-                vm(3, 2, 6 * G * nr, lanes),
+                edges(2 * G), edges(nr - 2 * G),
+                edges(2 * G), edges(nr - 2 * G),
                 vm(6, nr + 1, nt, lanes),
                 vm(6, nr, nt, lanes),
                 vm(2, 6, planes, nt, lanes),
@@ -536,12 +571,12 @@
                 vm(pad8(nr), lanes),
                 vm(pad8(nr), lanes),
                 vm(2, nt, lanes),
-                pltpu.SemaphoreType.DMA((3, 6)),
-                pltpu.SemaphoreType.DMA((3, 6)),
+                pltpu.SemaphoreType.DMA((3, 8)),
+                pltpu.SemaphoreType.DMA((3, 8)),
                 pltpu.SemaphoreType.DMA((2,)),
             ],
             compiler_params=pltpu.CompilerParams(
-                collective_id=0, has_side_effects=True, vmem_limit_bytes=24 * 1024 * 1024
+                collective_id=0, has_side_effects=True
             ),
         )(magnetic, electric)
 

time: 39.7 us -> 41.8 us (1.053)
  Pallas kernels: 35.6 us -> 38.6 us
  local copies, waits for them, and re-layouts: 3.35 us -> 2.46 us
    pallas_call x1, Pallas kernels: 35.6 us -> 38.6 us  [body(): pl.pallas_call(functools.partial(kernel, sizes), out_shape=[jax.ShapeDtyp...]
    unnamed x6 -> x4, local copies, waits for them, and re-layouts: 3.35 us -> 2.46 us
where the time goes in v3:
time: 41.8 us; the launch traced here: 41.7 us
  Pallas kernels  38.6 us (92%)
  local copies, waits for them, and re-layouts  2.46 us (6%)
  between operations  0.65 us (2%)
    pallas_call x1, Pallas kernels, body(): pl.pallas_call(functools.partial(kernel, sizes), out_shape=[jax.ShapeDtyp...  38.6 us
    unnamed x4, local copies, waits for them, and re-layouts  2.46 us

profile of v3, /device:TPU:0, one launch (start us, length us, event | category | flops | bytes accessed | tf_op | source)
XLA Modules:
  0.0 41.7 jit_solution(410135913180125981)
XLA Ops:
  0.6 38.6 %shard_map.41 = (f32[3,12,16,128]{3,2,1,0:T(8,128)}, f32[3,12,16,128]{3,2,1,0:T(8,128)}) custom-call(f32[3,12,16,128]{3,2,1,0:T(8,128)} %mag.1, f32[3,12,16,128]{3,2,1,0:T(8,128)} %ele.1), custom_call_target="tpu_custom_call" | custom-call | tf_op jit(solution)/shard_map/pallas_call | solution.py:550
  39.2 0.0 copy-start
  39.2 1.7 %copy.6 = f32[3,12,16,128]{3,2,1,0:T(8,128)} copy(f32[3,12,16,128]{3,2,1,0:T(8,128)} %get-tuple-element.4) | data formatting | bytes 589824
  41.0 0.0 copy-done
  41.0 0.7 %copy.7 = f32[3,12,16,128]{3,2,1,0:T(8,128)} copy(f32[3,12,16,128]{3,2,1,0:T(8,128)S(1)} %copy-done) | data formatting | bytes 589824
Async XLA Ops:
  39.2 1.8 %copy-start = (f32[3,12,16,128]{3,2,1,0:T(8,128)S(1)}, f32[3,12,16,128]{3,2,1,0:T(8,128)}, u32[]{:S(2)}) copy-start(f32[3,12,16,128]{3,2,1,0:T(8,128)} %get-tuple-element.5) | copy-start | bytes 884740

commit v4 on v2

--- a/solution.py
+++ b/solution.py
@@ -541,7 +541,7 @@
                 pltpu.SemaphoreType.DMA((2,)),
             ],
             compiler_params=pltpu.CompilerParams(
-                collective_id=0, has_side_effects=True, vmem_limit_bytes=24 * 1024 * 1024
+                collective_id=0, has_side_effects=True
             ),
         )(magnetic, electric)
 

time: 39.7 us -> 39.6 us (level)
  local copies, waits for them, and re-layouts: 3.35 us -> 2.46 us
  Pallas kernels: 35.6 us -> 36.3 us
    unnamed x6 -> x4, local copies, waits for them, and re-layouts: 3.35 us -> 2.46 us
    pallas_call x1, Pallas kernels: 35.6 us -> 36.3 us  [body(): pl.pallas_call(functools.partial(kernel, sizes), out_shape=[jax.ShapeDtyp...]
where the time goes in v4:
time: 39.6 us; the launch traced here: 39.4 us
  Pallas kernels  36.3 us (92%)
  local copies, waits for them, and re-layouts  2.46 us (6%)
  between operations  0.65 us (2%)
    pallas_call x1, Pallas kernels, body(): pl.pallas_call(functools.partial(kernel, sizes), out_shape=[jax.ShapeDtyp...  36.3 us
    unnamed x4, local copies, waits for them, and re-layouts  2.46 us

profile of v4, /device:TPU:0, one launch (start us, length us, event | category | flops | bytes accessed | tf_op | source)
XLA Modules:
  0.0 39.4 jit_solution(8025030144503415337)
XLA Ops:
  0.6 36.3 %shard_map.41 = (f32[3,12,16,128]{3,2,1,0:T(8,128)}, f32[3,12,16,128]{3,2,1,0:T(8,128)}) custom-call(f32[3,12,16,128]{3,2,1,0:T(8,128)} %mag.1, f32[3,12,16,128]{3,2,1,0:T(8,128)} %ele.1), custom_call_target="tpu_custom_call" | custom-call | tf_op jit(solution)/shard_map/pallas_call | solution.py:515
  36.9 0.0 copy-start
  36.9 1.7 %copy.6 = f32[3,12,16,128]{3,2,1,0:T(8,128)} copy(f32[3,12,16,128]{3,2,1,0:T(8,128)} %get-tuple-element.4) | data formatting | bytes 589824
  38.7 0.0 copy-done
  38.7 0.7 %copy.7 = f32[3,12,16,128]{3,2,1,0:T(8,128)} copy(f32[3,12,16,128]{3,2,1,0:T(8,128)S(1)} %copy-done) | data formatting | bytes 589824
Async XLA Ops:
  36.9 1.8 %copy-start = (f32[3,12,16,128]{3,2,1,0:T(8,128)S(1)}, f32[3,12,16,128]{3,2,1,0:T(8,128)}, u32[]{:S(2)}) copy-start(f32[3,12,16,128]{3,2,1,0:T(8,128)} %get-tuple-element.5) | copy-start | bytes 884740
